TPU v7x, 32 devices: a whole 2x2x4 slice. The times are simulated.
32 devices in a mesh: ta: 4 (over y, core), xyz: 8 (over z, x).
Axes of the slice: x: 2, y: 2, z: 4, core: 2. Of those that a mesh axis runs over, the one named last changes fastest.
Arguments:
- prop_one: bfloat16 [4, 2, 12, 12, 32768], P('ta', None, None, None, 'xyz'), may hold values from -1.796875 to 1.796875
- prop_two: bfloat16 [4, 2, 12, 12, 32768], P('ta', None, None, None, 'xyz'), may hold values from -1.796875 to 1.796875
Outputs:
- momentum_fields: float32 [4, 16, 2, 32768], P(None, 'ta', None, 'xyz')
All inputs are finite; a program needn't handle non-finite values.
Results may differ from a plain program's by a relative error of at most 0.0003.
Values sent between devices are 32-bit elements; how exact they have to be, the bound alone decides.
A program may use at most 128 MiB of HBM per device.

v0:
```python
import math

import jax
import jax.numpy as jnp
import numpy as np
from jax import lax
from jax.experimental import pallas as pl
from jax.experimental.pallas import tpu as pltpu
from jax.sharding import PartitionSpec as P

L = 32


spin_columns = [[3, 2, 1, 0], [3, 2, 1, 0], [2, 3, 0, 1], [2, 3, 0, 1]]
spin_phases = [[1j, 1j, -1j, -1j], [-1.0, 1.0, 1.0, -1.0], [1j, -1j, -1j, 1j], [1.0, 1.0, 1.0, 1.0]]
chiral_signs = [1.0, 1.0, -1.0, -1.0]


def vertex_parts():
    result = []
    for gamma_index in range(4):
        columns = spin_columns[gamma_index]
        phases = spin_phases[gamma_index]
        rows_list = [columns[a // 3] * 3 + a % 3 for a in range(12)]
        phase_list = [complex(phases[a // 3]) for a in range(12)]
        result.append((rows_list, phase_list))
    return (result, [chiral_signs[a // 3] for a in range(12)])


def contract(prop_a, prop_b):
    gammas, chirality = vertex_parts()
    left_real, left_imag, right_real, right_imag = ([], [], [], [])
    for rows_list, phase_list in gammas:
        pick_real = jnp.stack([prop_a[0, q] for q in rows_list])
        pick_imag = jnp.stack([prop_a[1, q] for q in rows_list])
        phase_real = jnp.asarray(np.array([p.real for p in phase_list]), jnp.bfloat16)[
            :, None, None
        ]
        phase_imag = jnp.asarray(np.array([p.imag for p in phase_list]), jnp.bfloat16)[
            :, None, None
        ]
        left_real.append(phase_real * pick_real - phase_imag * pick_imag)
        left_imag.append(phase_real * pick_imag + phase_imag * pick_real)
        col_real = jnp.stack([prop_b[0][:, q] for q in rows_list], axis=1)
        col_imag = jnp.stack([prop_b[1][:, q] for q in rows_list], axis=1)
        factor = np.array(
            [
                [phase_list[c] * chirality[rows_list[c]] * chirality[a] for c in range(12)]
                for a in range(12)
            ]
        )
        factor_real = jnp.asarray(factor.real, jnp.bfloat16)[:, :, None]
        factor_imag = jnp.asarray(factor.imag, jnp.bfloat16)[:, :, None]
        right_real.append(factor_real * col_real + factor_imag * col_imag)
        right_imag.append(factor_imag * col_real - factor_real * col_imag)
    left_rows = jnp.stack(left_real + left_imag).reshape(8, 144, -1)
    right_rows = jnp.stack(right_real + right_imag).reshape(8, 144, -1)
    products = jnp.einsum("mks,nks->mns", left_rows, right_rows, preferred_element_type=jnp.float32)
    real_sum = products[:4, :4] - products[4:, 4:]
    imag_sum = products[:4, 4:] + products[4:, :4]
    return jnp.stack([real_sum.reshape(16, -1), imag_sum.reshape(16, -1)], axis=1)


def dft_tables(length):
    positions = np.arange(length)
    turn_count = positions[:, None] * positions[None, :] % length
    angles = turn_count * (2.0 * math.pi / length)
    cosines = jnp.asarray(np.cos(angles) / math.sqrt(length), jnp.float32)
    sines = jnp.asarray(np.sin(angles) / math.sqrt(length), jnp.float32)
    return (cosines, sines)


def plane_dft(fields):
    cosines, sines = dft_tables(L)
    highest = lax.Precision.HIGHEST
    shape = fields.shape
    grid = fields.reshape(shape[:4] + (L, L))
    real_part = grid[:, :, 0]
    imag_part = grid[:, :, 1]

    def along_z(values, table):
        return jnp.einsum(
            "tfpyz,zk->tfpyk", values, table, precision=highest, preferred_element_type=jnp.float32
        )

    def along_y(values, table):
        return jnp.einsum(
            "tfpyz,yk->tfpkz", values, table, precision=highest, preferred_element_type=jnp.float32
        )

    mid_real = along_z(real_part, cosines) + along_z(imag_part, sines)
    mid_imag = along_z(imag_part, cosines) - along_z(real_part, sines)
    out_real = along_y(mid_real, cosines) + along_y(mid_imag, sines)
    out_imag = along_y(mid_imag, cosines) - along_y(mid_real, sines)
    return jnp.stack([out_real, out_imag], axis=2).reshape(shape)


def line_dft(data):
    length = data.shape[-2]
    cosines, sines = dft_tables(length)
    real_part = data[..., 0, :, :]
    imag_part = data[..., 1, :, :]

    def transform_rows(values, table):
        return jnp.einsum(
            "...xq,xk->...qk",
            values,
            table,
            precision=lax.Precision.HIGHEST,
            preferred_element_type=jnp.float32,
        )

    out_real = transform_rows(real_part, cosines) + transform_rows(imag_part, sines)
    out_imag = transform_rows(imag_part, cosines) - transform_rows(real_part, sines)
    stacked = jnp.stack([out_real, out_imag], axis=-3)
    return stacked.reshape(stacked.shape[:-2] + (stacked.shape[-2] * stacked.shape[-1],))


def on_device(prop_one, prop_two):
    fields = lax.map(
        lambda slice_pair: contract(slice_pair[0], slice_pair[1]), (prop_one, prop_two)
    )
    local_times, field_count, parts, slab = fields.shape
    planes = slab // (L * L)
    fields = plane_dft(fields.reshape(local_times, field_count, parts, planes, L * L))
    turned_fields = line_dft(lax.all_to_all(fields, "xyz", split_axis=4, concat_axis=3, tiled=True))
    result = lax.all_to_all(turned_fields, "ta", split_axis=1, concat_axis=0, tiled=True)
    return result

LANES = 128
GROUP_PERMS = (0, 2)


def spin_tables():
    chi = np.array(chiral_signs)
    alpha = np.array(spin_phases) * chi[None, :]
    beta = np.array([[spin_phases[n][c] * chi[spin_columns[n][c]] for c in range(4)] for n in range(4)])
    groups = []
    for pair, first in enumerate(GROUP_PERMS):
        found = []
        for a in range(4):
            for members in found:
                ratio = alpha[first : first + 2, a] / alpha[first : first + 2, members[0][0]]
                if ratio[0] == ratio[1] and ratio[0] in (1, -1):
                    members.append((a, int(ratio[0].real)))
                    break
            else:
                found.append([(a, 1)])
        assert len(found) == 2
        groups.append(found)
    mixer = np.zeros((2, 4, 4, 2, 2, 2, 2, 16))
    for mu in range(4):
        for nu in range(4):
            for half in range(2):
                lead = groups[mu // 2][half][0][0]
                for row in range(12):
                    m = alpha[mu, lead] * beta[nu, row // 3]
                    at = (mu // 2, half, nu // 2)
                    mixer[(0, mu, nu) + at + (0, row)] = m.real
                    mixer[(0, mu, nu) + at + (1, row)] = -m.imag
                    mixer[(1, mu, nu) + at + (0, row)] = m.imag
                    mixer[(1, mu, nu) + at + (1, row)] = m.real
    return groups, mixer.reshape(32, 256)


def complex_block(table):
    return np.block([[table.real, table.imag], [-table.imag, table.real]])


def high_low(table):
    high = np.asarray(table).astype(jnp.bfloat16)
    low = (table - high.astype(np.float64)).astype(jnp.bfloat16)
    return jnp.asarray(np.stack([high, low]))


def plane_tables(length):
    quarter = LANES // length
    outer = length // quarter
    lane = np.arange(LANES)
    y, z = lane // length, lane % length
    twiddle = np.exp(-2j * np.pi * np.outer(np.arange(outer), y) / length)
    ky, slot = lane // length, lane % length
    kz = (slot % outer) * quarter + slot // outer
    table = np.exp(-2j * np.pi * (np.outer(y, ky) / quarter + np.outer(z, kz) / length)) / length
    return (
        jnp.asarray(np.stack([twiddle.real, twiddle.imag]), jnp.float32),
        high_low(complex_block(table)),
    )


def line_table(length, own, sources):
    x = np.arange(length)
    turn = np.exp(-2j * np.pi * np.outer(x, x) / length) / math.sqrt(length)
    parts = complex_block(turn).reshape(2, sources, length // sources, 2, length)
    full = np.einsum("asxbk,fg->sxafbgk", parts, np.eye(own))
    rows = length * 2 * own
    return high_low(full.reshape(rows, rows))


def split_dot(values, table):
    high = values.astype(jnp.bfloat16)
    low = (values - high.astype(jnp.float32)).astype(jnp.bfloat16)

    def dot(a, b):
        return jnp.dot(a, b, preferred_element_type=jnp.float32)

    return dot(high, table[0]) + (dot(low, table[0]) + dot(high, table[1]))


def small_fft(values):
    count = len(values)
    if count == 1:
        return values
    even, odd = small_fft(values[0::2]), small_fft(values[1::2])
    low, high = [], []
    for k in range(count // 2):
        re, im = odd[k]
        if k == 0:
            pass
        elif 4 * k == count:
            re, im = im, -re
        else:
            c, s = math.cos(2 * math.pi * k / count), math.sin(2 * math.pi * k / count)
            re, im = c * re + s * im, c * im - s * re
        low.append((even[k][0] + re, even[k][1] + im))
        high.append((even[k][0] - re, even[k][1] - im))
    return low + high


def swap_blocks(values):
    width = LANES // 4
    shape = values[0].shape
    block = lax.broadcasted_iota(jnp.int32, shape, len(shape) - 1) // width
    axis = len(shape) - 1
    values = list(values)
    for step in (2, 1):
        keep = (block // step) % 2 == 0
        result = [None] * 4
        for i in range(4):
            if (i // step) % 2 == 0:
                a, b = values[i], values[i + step]
                result[i] = jnp.where(keep, a, pltpu.roll(b, step * width, axis))
                result[i + step] = jnp.where(keep, pltpu.roll(a, LANES - step * width, axis), b)
        values = result
    return values


def partial_sums(tile, zero, groups, one_ref, two_ref, ring, turned, high_ref, low_ref):
    lanes = pl.ds(pl.multiple_of(tile * LANES, LANES), LANES)
    spin = lax.broadcasted_iota(jnp.int32, (12, LANES), 0) // 3
    even = spin % 2 == 0
    for part in range(2):
        for row in range(12):
            value = two_ref[0, part, row, :, lanes].astype(jnp.float32)
            slot = part * 12 + row
            ring[slot, pl.ds(0, 12), :] = value
            ring[slot, pl.ds(zero + 12, 12), :] = value
    for part in range(2):
        for row in range(12):
            slot = part * 12 + row
            third = ring[slot, pl.ds(zero + 9, 12), :]
            first = ring[slot, pl.ds(zero + 3, 12), :]
            turned[0, slot, :, :] = jnp.where(even, third, first)
            turned[1, slot, :, :] = ring[slot, pl.ds(zero + 6, 12), :]
    for pair in range(2):
        columns = spin_columns[GROUP_PERMS[pair]]
        for half in range(2):
            sums = [[None, None], [None, None]]
            for a, sign in groups[pair][half]:
                for colour in range(3):
                    left = columns[a] * 3 + colour
                    right = a * 3 + colour
                    ar = one_ref[0, 0, left, :, lanes].astype(jnp.float32)
                    ai = one_ref[0, 1, left, :, lanes].astype(jnp.float32)
                    for turn in range(2):
                        br = turned[turn, right, :, :]
                        bi = turned[turn, 12 + right, :, :]
                        re = ar * br + ai * bi
                        im = ai * br - ar * bi
                        for at, term in enumerate((re, im)):
                            old = sums[turn][at]
                            if old is None:
                                sums[turn][at] = term
                            elif sign > 0:
                                sums[turn][at] = old + term
                            else:
                                sums[turn][at] = old - term
            for turn in range(2):
                for at in range(2):
                    start = (((pair * 2 + half) * 2 + turn) * 2 + at) * 16
                    total = jnp.concatenate([sums[turn][at], jnp.zeros((4, LANES), jnp.float32)], axis=0)
                    high = total.astype(jnp.bfloat16)
                    high_ref[start : start + 16, lanes] = high
                    low_ref[start : start + 16, lanes] = (total - high.astype(jnp.float32)).astype(jnp.bfloat16)


def plane_blocks(mixer_ref, twiddle_ref, plane_ref, high_ref, low_ref, tiles, store):
    mixer = mixer_ref[...]
    fields = jnp.dot(mixer, high_ref[...], preferred_element_type=jnp.float32) + jnp.dot(
        mixer, low_ref[...], preferred_element_type=jnp.float32
    )
    blocks = [fields[:, t * LANES : (t + 1) * LANES] for t in range(tiles)]
    spectrum = small_fft([(block[:16], block[16:]) for block in blocks])
    turned = []
    for k, (re, im) in enumerate(spectrum):
        c = twiddle_ref[0, k : k + 1, :]
        s = twiddle_ref[1, k : k + 1, :]
        turned.append(jnp.concatenate([re * c - im * s, re * s + im * c], axis=1) if k else jnp.concatenate([re, im], axis=1))
    out = split_dot(jnp.concatenate(turned, axis=0), plane_ref)
    upper = lax.broadcasted_iota(jnp.int32, (8, LANES), 0) < 4
    for half in range(tiles // 4):
        parts = []
        for part in range(2):
            rows = [
                out[(4 * half + p) * 16 : (4 * half + p + 1) * 16, part * LANES : (part + 1) * LANES]
                for p in range(4)
            ]
            parts.append(swap_blocks(rows))
        for k in range(4):
            owner = k * (tiles // 4) + half
            for pair in range(2):
                re = parts[0][k][pair * 8 : pair * 8 + 8]
                im = parts[1][k][pair * 8 : pair * 8 + 8]
                store(owner, 2 * pair, jnp.where(upper, re, pltpu.roll(im, 4, 0)))
                store(owner, 2 * pair + 1, jnp.where(upper, pltpu.roll(re, 4, 0), im))


def finish_time(rows, line_ref, out_ref, at, own):
    out = split_dot(rows.T, line_ref)
    for part in range(2):
        grid = out[:, part * LANES : (part + 1) * LANES].reshape(4, 4, 8, LANES)
        done = swap_blocks([grid[:, q].reshape(32, LANES) for q in range(4)])
        for f in range(own):
            out_ref[at, f, pl.ds(part, 32, stride=2), :] = done[f]


def send_kernel(groups, tiles, one_ref, two_ref, mixer_ref, twiddle_ref, plane_ref, out_ref, ring, turned, high_ref, low_ref):
    zero = jnp.minimum(pl.program_id(0), 0)

    @pl.loop(0, tiles)
    def _(tile):
        partial_sums(tile, zero, groups, one_ref, two_ref, ring, turned, high_ref, low_ref)

    def store(owner, group, value):
        out_ref[owner, group, 0, :, :] = value

    plane_blocks(mixer_ref, twiddle_ref, plane_ref, high_ref, low_ref, tiles, store)


def receive_kernel(times, sources, planes, own, got_ref, line_ref, out_ref):
    for t in range(times):
        rows = got_ref[:, t].reshape(sources * planes * 8, LANES)
        finish_time(rows, line_ref, out_ref, t, own)


def fast_device(prop_one, prop_two, times, sources):
    slab = prop_one.shape[-1]
    plane = L * L
    planes, tiles = slab // plane, plane // LANES
    own = 16 // times
    groups, mixer = spin_tables()
    twiddle, plane_table = plane_tables(L)
    block = pl.BlockSpec((1, 2, 12, 12, plane), lambda x: (0, 0, 0, 0, x))

    def whole(array):
        return pl.BlockSpec(array.shape, lambda x: (0,) * array.ndim)

    mixer = jnp.asarray(mixer, jnp.bfloat16)
    sent = pl.pallas_call(
        lambda *refs: send_kernel(groups, tiles, *refs),
        grid=(planes,),
        out_shape=jax.ShapeDtypeStruct((sources, times, planes, 8, LANES), jnp.float32),
        in_specs=[block, block, whole(mixer), whole(twiddle), whole(plane_table)],
        out_specs=pl.BlockSpec((sources, times, 1, 8, LANES), lambda x: (0, 0, x, 0, 0)),
        scratch_shapes=[
            pltpu.VMEM((24, 24, LANES), jnp.float32),
            pltpu.VMEM((2, 24, 12, LANES), jnp.float32),
            pltpu.VMEM((256, plane), jnp.bfloat16),
            pltpu.VMEM((256, plane), jnp.bfloat16),
        ],
    )(prop_one, prop_two, mixer, twiddle, plane_table)
    got = lax.all_to_all(sent, "xyz", split_axis=0, concat_axis=0, tiled=True)
    got = lax.all_to_all(got, "ta", split_axis=1, concat_axis=1, tiled=True)
    table = line_table(L, own, sources)
    out = pl.pallas_call(
        lambda *refs: receive_kernel(times, sources, planes, own, *refs),
        out_shape=jax.ShapeDtypeStruct((times, own, slab * 2 // LANES, LANES), jnp.float32),
    )(got, table)
    return out.reshape(times, own, slab // LANES, 2, LANES).transpose(0, 1, 3, 2, 4).reshape(times, own, 2, slab)


def solution(mesh):
    placed = (P("ta", None, None, None, "xyz"), P("ta", None, None, None, "xyz"))
    times, sources = mesh.shape["ta"], mesh.shape["xyz"]

    def device(prop_one, prop_two):
        planes = prop_one.shape[-1] // (L * L)
        fits = 4 * L == LANES and planes * sources == L and L // sources == 4 and times == 4
        if fits and prop_one.shape[0] == 1:
            return fast_device(prop_one, prop_two, times, sources)
        return on_device(prop_one, prop_two)

    return jax.shard_map(
        device, mesh=mesh, in_specs=placed, out_specs=P(None, "ta", None, "xyz"), check_vma=False
    )
```

profile of v0, /device:TPU:0, one launch (start us, length us, event | category | flops | bytes accessed | tf_op | source)
XLA Modules:
  0.0 57.1 jit_solution(17012801455321791077)
XLA Ops:
  0.0 0.0 copy-start
  0.0 5.2 %copy.10.refs_0_ = bf16[1,2,12,12,4096]{4,3,2,1,0:T(8,128)(2,1)} copy(bf16[1,2,12,12,4096]{4,1,3,2,0:T(2,128)(2,1)} %param.6) | data formatting | bytes 4718592 | tf_op args[0]
  5.2 0.0 copy-done
  5.2 3.4 %copy.11.refs_1_ = bf16[1,2,12,12,4096]{4,3,2,1,0:T(8,128)(2,1)} copy(bf16[1,2,12,12,4096]{4,1,3,2,0:T(2,128)(2,1)S(1)} %copy-done) | data formatting | bytes 4718592 | tf_op args[1]
  8.7 11.7 %shard_map.64 = f32[8,4,4,8,128]{4,3,2,1,0:T(8,128)} custom-call(bf16[1,2,12,12,4096]{4,3,2,1,0:T(8,128)(2,1)} %copy.10.refs_0_, bf16[1,2,12,12,4096]{4,3,2,1,0:T(8,128)(2,1)} %copy.11.refs_1_, bf16[32,256]{1,0:T(8,128)(2,1)} %constant.10.clone.refs_2_, f32[2,8,128]{2,1,0:T(8,128)} %constant.8.clone.refs_3_, bf16[2,256,256]{2,1,0:T(8,128)(2,1)} %constant.9.clone.refs_4_), custom_call_target="tpu_custom_call" | custom-call | tf_op jit(solution)/shard_map/pallas_call | solution.py:369
  20.4 21.8 %all_to_all.10 = f32[8,4,4,8,128]{4,3,2,1,0:T(8,128)S(1)} all-to-all(f32[8,4,4,8,128]{4,3,2,1,0:T(8,128)} %shard_map.64), channel_id=1, replica_groups=mesh['ta'=4,'xyz'=8] {'xyz'}, dimensions={0} | all-to-all | bytes 1048576 | tf_op jit(solution)/shard_map/all_to_all | solution.py:382
  42.2 11.4 %all_to_all.11 = f32[8,4,4,8,128]{4,3,2,0,1:T(8,128)S(1)} all-to-all(f32[8,4,4,8,128]{4,3,2,0,1:T(8,128)S(1)} %copy.12), channel_id=1, replica_groups=mesh['ta'=4,'xyz'=8] {'ta'}, dimensions={1} | all-to-all | bytes 1048576 | tf_op jit(solution)/shard_map/all_to_all | solution.py:383
  53.6 0.8 %copy.13.refs_0_ = f32[8,4,4,8,128]{4,3,2,1,0:T(8,128)} copy(f32[8,4,4,8,128]{4,3,2,0,1:T(8,128)S(1)} %all_to_all.11) | data formatting | bytes 1048576 | tf_op jit(solution)/shard_map/all_to_all | solution.py:383
  54.5 2.6 %shard_map.65 = f32[4,4,64,128]{3,2,1,0:T(8,128)} custom-call(f32[8,4,4,8,128]{4,3,2,1,0:T(8,128)} %copy.13.refs_0_, bf16[2,256,256]{2,1,0:T(8,128)(2,1)} %constant.11.clone.refs_1_), custom_call_target="tpu_custom_call" | custom-call | tf_op jit(solution)/shard_map/pallas_call | solution.py:385
  (1 shorter events, 0.0 us)
Async XLA Ops:
  0.0 5.2 %copy-start = (bf16[1,2,12,12,4096]{4,1,3,2,0:T(2,128)(2,1)S(1)}, bf16[1,2,12,12,4096]{4,1,3,2,0:T(2,128)(2,1)}, u32[]{:S(2)}) copy-start(bf16[1,2,12,12,4096]{4,1,3,2,0:T(2,128)(2,1)} %param.7) | copy-start | bytes 7077892
where the time goes:
time: 57.3 us; the launch traced here: 57.1 us
  blocking collectives  33.2 us (58%)
  Pallas kernels  14.3 us (25%)
  local copies, waits for them, and re-layouts  9.55 us (17%)
    all_to_all x1, blocking collectives, fast_device(): got = lax.all_to_all(sent, 'xyz', split_axis=0, concat_axis=0, tiled=True)  21.8 us
    pallas_call x1, Pallas kernels, fast_device(): pl.pallas_call(lambda *refs: send_kernel(groups, tiles, *refs), grid=(pla...  11.7 us
    all_to_all x1, blocking collectives, fast_device(): got = lax.all_to_all(got, 'ta', split_axis=1, concat_axis=1, tiled=True)  11.4 us
    unnamed x4, local copies, waits for them, and re-layouts  8.69 us
    pallas_call x1, Pallas kernels, fast_device(): pl.pallas_call(lambda *refs: receive_kernel(times, sources, planes, own,...  2.61 us

commit v1 on v0

--- a/solution.py
+++ b/solution.py
@@ -1,3 +1,4 @@
+import functools
 import math
 
 import jax
@@ -135,32 +136,27 @@
     chi = np.array(chiral_signs)
     alpha = np.array(spin_phases) * chi[None, :]
     beta = np.array([[spin_phases[n][c] * chi[spin_columns[n][c]] for c in range(4)] for n in range(4)])
-    groups = []
-    for pair, first in enumerate(GROUP_PERMS):
-        found = []
-        for a in range(4):
-            for members in found:
-                ratio = alpha[first : first + 2, a] / alpha[first : first + 2, members[0][0]]
-                if ratio[0] == ratio[1] and ratio[0] in (1, -1):
-                    members.append((a, int(ratio[0].real)))
-                    break
-            else:
-                found.append([(a, 1)])
-        assert len(found) == 2
-        groups.append(found)
-    mixer = np.zeros((2, 4, 4, 2, 2, 2, 2, 16))
-    for mu in range(4):
-        for nu in range(4):
-            for half in range(2):
-                lead = groups[mu // 2][half][0][0]
-                for row in range(12):
-                    m = alpha[mu, lead] * beta[nu, row // 3]
-                    at = (mu // 2, half, nu // 2)
-                    mixer[(0, mu, nu) + at + (0, row)] = m.real
-                    mixer[(0, mu, nu) + at + (1, row)] = -m.imag
-                    mixer[(1, mu, nu) + at + (0, row)] = m.imag
-                    mixer[(1, mu, nu) + at + (1, row)] = m.real
-    return groups, mixer.reshape(32, 256)
+    tables = []
+    for phases in (alpha, beta):
+        pairs = []
+        for first in GROUP_PERMS:
+            found = []
+            for a in range(4):
+                for members in found:
+                    ratio = phases[first : first + 2, a] / phases[first : first + 2, members[0][0]]
+                    if ratio[0] == ratio[1] and ratio[0] in (1, -1):
+                        members.append((a, int(ratio[0].real)))
+                        break
+                else:
+                    found.append([(a, 1)])
+            assert len(found) == 2
+            pairs.append(found)
+        lead = np.array([[phases[m, pairs[m // 2][half][0][0]] for half in range(2)] for m in range(4)])
+        signs = np.array([[int((lead[m, half] / lead[m, 0]).real) for half in range(2)] for m in range(4)])
+        tables.append((pairs, lead[:, 0], signs))
+    left, right = tables
+    phase = np.outer(left[1], right[1]).reshape(16)
+    return left[0], left[2], right[0], right[2], phase
 
 
 def complex_block(table):
@@ -245,62 +241,66 @@
     return values
 
 
-def partial_sums(tile, zero, groups, one_ref, two_ref, ring, turned, high_ref, low_ref):
-    lanes = pl.ds(pl.multiple_of(tile * LANES, LANES), LANES)
-    spin = lax.broadcasted_iota(jnp.int32, (12, LANES), 0) // 3
-    even = spin % 2 == 0
-    for part in range(2):
-        for row in range(12):
-            value = two_ref[0, part, row, :, lanes].astype(jnp.float32)
-            slot = part * 12 + row
-            ring[slot, pl.ds(0, 12), :] = value
-            ring[slot, pl.ds(zero + 12, 12), :] = value
-    for part in range(2):
-        for row in range(12):
-            slot = part * 12 + row
-            third = ring[slot, pl.ds(zero + 9, 12), :]
-            first = ring[slot, pl.ds(zero + 3, 12), :]
-            turned[0, slot, :, :] = jnp.where(even, third, first)
-            turned[1, slot, :, :] = ring[slot, pl.ds(zero + 6, 12), :]
+def add_signed(total, term, sign):
+    if total is None:
+        return term if sign > 0 else -term
+    return total + term if sign > 0 else total - term
+
+
+def site_sums(tables, one_ref, two_ref, wide, turned, mixed):
+    left_groups, left_signs, right_groups, right_signs, _ = tables
+    rows = one_ref.shape[2]
+    even = lax.broadcasted_iota(jnp.int32, (8, LANES), 0) % 2 == 0
+
+    @pl.loop(0, 12)
+    def _(a):
+        for c in range(12):
+            value = two_ref[a, c, :, :].astype(jnp.float32)
+            wide[a, c, :, :] = value
+            for at in range(0, rows, 8):
+                piece = value[at : at + 8]
+                turned[a, c, at : at + 8, :] = jnp.where(even, pltpu.roll(piece, 7, 0), pltpu.roll(piece, 1, 0))
+
     for pair in range(2):
-        columns = spin_columns[GROUP_PERMS[pair]]
+        left_columns = spin_columns[GROUP_PERMS[pair]]
+        sums = {}
         for half in range(2):
-            sums = [[None, None], [None, None]]
-            for a, sign in groups[pair][half]:
-                for colour in range(3):
-                    left = columns[a] * 3 + colour
-                    right = a * 3 + colour
-                    ar = one_ref[0, 0, left, :, lanes].astype(jnp.float32)
-                    ai = one_ref[0, 1, left, :, lanes].astype(jnp.float32)
-                    for turn in range(2):
-                        br = turned[turn, right, :, :]
-                        bi = turned[turn, 12 + right, :, :]
-                        re = ar * br + ai * bi
-                        im = ai * br - ar * bi
-                        for at, term in enumerate((re, im)):
-                            old = sums[turn][at]
-                            if old is None:
-                                sums[turn][at] = term
-                            elif sign > 0:
-                                sums[turn][at] = old + term
-                            else:
-                                sums[turn][at] = old - term
             for turn in range(2):
-                for at in range(2):
-                    start = (((pair * 2 + half) * 2 + turn) * 2 + at) * 16
-                    total = jnp.concatenate([sums[turn][at], jnp.zeros((4, LANES), jnp.float32)], axis=0)
-                    high = total.astype(jnp.bfloat16)
-                    high_ref[start : start + 16, lanes] = high
-                    low_ref[start : start + 16, lanes] = (total - high.astype(jnp.float32)).astype(jnp.bfloat16)
-
-
-def plane_blocks(mixer_ref, twiddle_ref, plane_ref, high_ref, low_ref, tiles, store):
-    mixer = mixer_ref[...]
-    fields = jnp.dot(mixer, high_ref[...], preferred_element_type=jnp.float32) + jnp.dot(
-        mixer, low_ref[...], preferred_element_type=jnp.float32
-    )
-    blocks = [fields[:, t * LANES : (t + 1) * LANES] for t in range(tiles)]
-    spectrum = small_fft([(block[:16], block[16:]) for block in blocks])
+                right_columns = spin_columns[GROUP_PERMS[turn]]
+                for side in range(2):
+                    straight, crossed = None, None
+                    for a, left_sign in left_groups[pair][half]:
+                        for c, right_sign in right_groups[turn][side]:
+                            for i in range(3):
+                                for j in range(3):
+                                    sink, source = left_columns[a] * 3 + i, c * 3 + j
+                                    first = one_ref[sink, source, :, :].astype(jnp.float32)
+                                    at = (a * 3 + i, right_columns[c] * 3 + j)
+                                    sign = left_sign * right_sign
+                                    straight = add_signed(straight, first * wide[at[0], at[1], :, :], sign)
+                                    crossed = add_signed(crossed, first * turned[at[0], at[1], :, :], sign)
+                    sums[half, turn, side] = (straight, crossed)
+        for mu in (2 * pair, 2 * pair + 1):
+            for nu in range(4):
+                for kind in range(2):
+                    total = None
+                    for half in range(2):
+                        for side in range(2):
+                            sign = int(left_signs[mu][half] * right_signs[nu][side])
+                            total = add_signed(total, sums[half, nu // 2, side][kind], sign)
+                    start = (4 * mu + nu) * rows
+                    mixed[kind, start : start + rows, :] = total
+
+
+def plane_blocks(phase_ref, twiddle_ref, plane_ref, mixed, tiles, store):
+    blocks = []
+    for t in range(tiles):
+        straight = [mixed[0, pl.ds(2 * t + part, 16, stride=2 * tiles), :] for part in range(2)]
+        crossed = [mixed[1, pl.ds(2 * t + part, 16, stride=2 * tiles), :] for part in range(2)]
+        re, im = straight[0] + straight[1], crossed[1] - crossed[0]
+        c, s = phase_ref[0], phase_ref[1]
+        blocks.append((c * re - s * im, c * im + s * re))
+    spectrum = small_fft(blocks)
     turned = []
     for k, (re, im) in enumerate(spectrum):
         c = twiddle_ref[0, k : k + 1, :]
@@ -334,23 +334,78 @@
             out_ref[at, f, pl.ds(part, 32, stride=2), :] = done[f]
 
 
-def send_kernel(groups, tiles, one_ref, two_ref, mixer_ref, twiddle_ref, plane_ref, out_ref, ring, turned, high_ref, low_ref):
-    zero = jnp.minimum(pl.program_id(0), 0)
-
-    @pl.loop(0, tiles)
-    def _(tile):
-        partial_sums(tile, zero, groups, one_ref, two_ref, ring, turned, high_ref, low_ref)
+def fused_kernel(
+    tables, tiles, planes, times, sources, own, names,
+    one_ref, two_ref, phase_ref, twiddle_ref, plane_ref, line_ref, out_ref,
+    wide, turned, mixed, send, got, send_sem, recv_sem,
+):
+    step = pl.program_id(0)
+    t, s = lax.axis_index(names[0]), lax.axis_index(names[1])
+    far = sorted(range(sources), key=lambda o: -min(o, sources - o))
+    offsets = [(a, o) for o in far for a in reversed(range(times)) if (a, o) != (0, 0)]
+    barrier = pltpu.get_barrier_semaphore()
+
+    def peer(a, o):
+        return lax.rem(t + a, times), lax.rem(s + o, sources)
+
+    def copy(x, k):
+        to_t, to_s = peer(*offsets[k])
+        return pltpu.make_async_remote_copy(
+            src_ref=send.at[to_s, to_t, x],
+            dst_ref=got.at[t, s, x],
+            send_sem=send_sem.at[x, k],
+            recv_sem=recv_sem.at[x, k],
+            device_id={names[0]: to_t, names[1]: to_s},
+            device_id_type=pl.DeviceIdType.MESH,
+        )
+
+    def arrival(x, k):
+        a, o = offsets[k]
+        from_t, from_s = peer(times - a, sources - o)
+        return pltpu.make_async_remote_copy(
+            src_ref=send.at[from_s, from_t, x],
+            dst_ref=got.at[from_t, from_s, x],
+            send_sem=send_sem.at[x, k],
+            recv_sem=recv_sem.at[x, k],
+            device_id={names[0]: from_t, names[1]: from_s},
+            device_id_type=pl.DeviceIdType.MESH,
+        )
+
+    @pl.when(step == 0)
+    def _():
+        for a, o in offsets:
+            to_t, to_s = peer(a, o)
+            pl.semaphore_signal(
+                barrier, inc=1, device_id={names[0]: to_t, names[1]: to_s}, device_id_type=pl.DeviceIdType.MESH
+            )
+
+    site_sums(tables, one_ref, two_ref, wide, turned, mixed)
 
     def store(owner, group, value):
-        out_ref[owner, group, 0, :, :] = value
-
-    plane_blocks(mixer_ref, twiddle_ref, plane_ref, high_ref, low_ref, tiles, store)
-
-
-def receive_kernel(times, sources, planes, own, got_ref, line_ref, out_ref):
-    for t in range(times):
-        rows = got_ref[:, t].reshape(sources * planes * 8, LANES)
-        finish_time(rows, line_ref, out_ref, t, own)
+        send[owner, group, step, :, :] = value
+
+    plane_blocks(phase_ref, twiddle_ref, plane_ref, mixed, tiles, store)
+
+    @pl.when(step == 0)
+    def _():
+        pl.semaphore_wait(barrier, len(offsets))
+
+    for k in range(len(offsets)):
+        copy(step, k).start()
+    got[t, s, step, :, :] = send[s, t, step, :, :]
+
+    @pl.when(step == planes - 1)
+    def _():
+        for a in range(times):
+            @pl.loop(0, planes)
+            def _(x):
+                for k in range(len(offsets)):
+                    if offsets[k][0] == a:
+                        arrival(x, k).wait_recv()
+                        copy(x, k).wait_send()
+            from_t = lax.rem(t + times - a, times)
+            rows = got[from_t].reshape(sources * planes * 8, LANES)
+            finish_time(rows, line_ref, out_ref, from_t, own)
 
 
 def fast_device(prop_one, prop_two, times, sources):
@@ -358,34 +413,42 @@
     plane = L * L
     planes, tiles = slab // plane, plane // LANES
     own = 16 // times
-    groups, mixer = spin_tables()
+    tables = spin_tables()
     twiddle, plane_table = plane_tables(L)
-    block = pl.BlockSpec((1, 2, 12, 12, plane), lambda x: (0, 0, 0, 0, x))
-
-    def whole(array):
-        return pl.BlockSpec(array.shape, lambda x: (0,) * array.ndim)
-
-    mixer = jnp.asarray(mixer, jnp.bfloat16)
-    sent = pl.pallas_call(
-        lambda *refs: send_kernel(groups, tiles, *refs),
+    line = line_table(L, own, sources)
+    phase = np.broadcast_to(tables[4][:, None], (16, LANES))
+    phase = jnp.asarray(np.stack([phase.real, phase.imag]), jnp.float32)
+
+    def paired(prop):
+        split = prop.reshape(2, 12, 12, slab // LANES, LANES).transpose(1, 2, 3, 0, 4)
+        return split.reshape(12, 12, slab // LANES * 2, LANES)
+
+    block = pl.BlockSpec((12, 12, 2 * tiles, LANES), lambda x: (0, 0, x, 0))
+
+    def whole(shape):
+        return pl.BlockSpec(shape, lambda x: (0,) * len(shape))
+
+    peers = times * sources - 1
+    shape = (times, own, slab * 2 // LANES, LANES)
+    out = pl.pallas_call(
+        functools.partial(fused_kernel, tables, tiles, planes, times, sources, own, ("ta", "xyz")),
         grid=(planes,),
-        out_shape=jax.ShapeDtypeStruct((sources, times, planes, 8, LANES), jnp.float32),
-        in_specs=[block, block, whole(mixer), whole(twiddle), whole(plane_table)],
-        out_specs=pl.BlockSpec((sources, times, 1, 8, LANES), lambda x: (0, 0, x, 0, 0)),
+        out_shape=jax.ShapeDtypeStruct(shape, jnp.float32),
+        in_specs=[block, block] + [whole(v.shape) for v in (phase, twiddle, plane_table, line)],
+        out_specs=whole(shape),
         scratch_shapes=[
-            pltpu.VMEM((24, 24, LANES), jnp.float32),
-            pltpu.VMEM((2, 24, 12, LANES), jnp.float32),
-            pltpu.VMEM((256, plane), jnp.bfloat16),
-            pltpu.VMEM((256, plane), jnp.bfloat16),
+            pltpu.VMEM((12, 12, 2 * tiles, LANES), jnp.float32),
+            pltpu.VMEM((12, 12, 2 * tiles, LANES), jnp.float32),
+            pltpu.VMEM((2, 16 * 2 * tiles, LANES), jnp.float32),
+            pltpu.VMEM((sources, times, planes, 8, LANES), jnp.float32),
+            pltpu.VMEM((times, sources, planes, 8, LANES), jnp.float32),
+            pltpu.SemaphoreType.DMA((planes, peers)),
+            pltpu.SemaphoreType.DMA((planes, peers)),
         ],
-    )(prop_one, prop_two, mixer, twiddle, plane_table)
-    got = lax.all_to_all(sent, "xyz", split_axis=0, concat_axis=0, tiled=True)
-    got = lax.all_to_all(got, "ta", split_axis=1, concat_axis=1, tiled=True)
-    table = line_table(L, own, sources)
-    out = pl.pallas_call(
-        lambda *refs: receive_kernel(times, sources, planes, own, *refs),
-        out_shape=jax.ShapeDtypeStruct((times, own, slab * 2 // LANES, LANES), jnp.float32),
-    )(got, table)
+        compiler_params=pltpu.CompilerParams(
+            collective_id=0, has_side_effects=True, dimension_semantics=("arbitrary",)
+        ),
+    )(paired(prop_one), paired(prop_two), phase, twiddle, plane_table, line)
     return out.reshape(times, own, slab // LANES, 2, LANES).transpose(0, 1, 3, 2, 4).reshape(times, own, 2, slab)
 
 

time: 57.3 us -> 27.9 us (0.49)
  blocking collectives: 33.2 us -> 0 us
  Pallas kernels: 14.3 us -> 25.8 us
  local copies, waits for them, and re-layouts: 9.55 us -> 1.89 us
    all_to_all x2 -> x0, blocking collectives: 33.2 us -> none  [the longest x1 21.8 us: fast_device(): got = lax.all_to_all(sent, 'xyz', split_axis=0, concat_axis=0, tiled=True)]
    pallas_call x2 -> x1, Pallas kernels: 14.3 us -> 25.8 us  [fast_device(): pl.pallas_call(functools.partial(fused_kernel, tables, tiles, planes, tim...]
    unnamed x4 -> x1, local copies, waits for them, and re-layouts: 8.69 us -> 1.89 us
    all_to_all x2 -> x0, local copies, waits for them, and re-layouts: 0.86 us -> none  [the longest x1 0.83 us: fast_device(): got = lax.all_to_all(got, 'ta', split_axis=1, concat_axis=1, tiled=True)]
where the time goes in v1:
time: 27.9 us; the launch traced here: 27.7 us
  Pallas kernels  25.8 us (92%)
  local copies, waits for them, and re-layouts  1.89 us (7%)
    pallas_call x1, Pallas kernels, fast_device(): pl.pallas_call(functools.partial(fused_kernel, tables, tiles, planes, tim...  25.8 us
    unnamed x1, local copies, waits for them, and re-layouts  1.89 us

profile of v1, /device:TPU:0, one launch (start us, length us, event | category | flops | bytes accessed | tf_op | source)
XLA Modules:
  0.0 27.7 jit_solution(16564744312796976526)
XLA Ops:
  0.0 25.8 %shard_map.64 = f32[4,4,64,128]{3,2,1,0:T(8,128)} custom-call(bf16[12,12,64,128]{3,2,1,0:T(8,128)(2,1)} %bitcast.15, bf16[12,12,64,128]{3,2,1,0:T(8,128)(2,1)} %bitcast.16, f32[2,16,128]{2,1,0:T(8,128)} %constant.11.clone.phase_ref, f32[2,8,128]{2,1,0:T(8,128)} %constant.8.clone.twiddle_ref, bf16[2,256,256]{2,1,0:T(8,128)(2,1)} %constant.9.clone.plane_ref, ...), custom_call_target="tpu_custom_call" | custom-call | tf_op jit(solution)/shard_map/pallas_call | solution.py:433
  25.8 1.9 %copy.11 = f32[4,4,2,4096]{3,2,1,0:T(2,128)} copy(f32[4,4,2,4096]{3,2,1,0:T(2,128)} %bitcast.17) | data formatting | bytes 1048576

commit v2 on v1

--- a/solution.py
+++ b/solution.py
@@ -342,31 +342,31 @@
     step = pl.program_id(0)
     t, s = lax.axis_index(names[0]), lax.axis_index(names[1])
     far = sorted(range(sources), key=lambda o: -min(o, sources - o))
-    offsets = [(a, o) for o in far for a in reversed(range(times)) if (a, o) != (0, 0)]
+    offsets = [(a, o) for a in range(times) for o in far if (a, o) != (0, 0)]
     barrier = pltpu.get_barrier_semaphore()
 
     def peer(a, o):
         return lax.rem(t + a, times), lax.rem(s + o, sources)
 
-    def copy(x, k):
+    def copy(k):
         to_t, to_s = peer(*offsets[k])
         return pltpu.make_async_remote_copy(
-            src_ref=send.at[to_s, to_t, x],
-            dst_ref=got.at[t, s, x],
-            send_sem=send_sem.at[x, k],
-            recv_sem=recv_sem.at[x, k],
+            src_ref=send.at[to_s, to_t],
+            dst_ref=got.at[t, s],
+            send_sem=send_sem.at[k],
+            recv_sem=recv_sem.at[k],
             device_id={names[0]: to_t, names[1]: to_s},
             device_id_type=pl.DeviceIdType.MESH,
         )
 
-    def arrival(x, k):
+    def arrival(k):
         a, o = offsets[k]
         from_t, from_s = peer(times - a, sources - o)
         return pltpu.make_async_remote_copy(
-            src_ref=send.at[from_s, from_t, x],
-            dst_ref=got.at[from_t, from_s, x],
-            send_sem=send_sem.at[x, k],
-            recv_sem=recv_sem.at[x, k],
+            src_ref=send.at[from_s, from_t],
+            dst_ref=got.at[from_t, from_s],
+            send_sem=send_sem.at[k],
+            recv_sem=recv_sem.at[k],
             device_id={names[0]: from_t, names[1]: from_s},
             device_id_type=pl.DeviceIdType.MESH,
         )
@@ -386,26 +386,21 @@
 
     plane_blocks(phase_ref, twiddle_ref, plane_ref, mixed, tiles, store)
 
-    @pl.when(step == 0)
+    @pl.when(step == planes - 1)
     def _():
         pl.semaphore_wait(barrier, len(offsets))
-
-    for k in range(len(offsets)):
-        copy(step, k).start()
-    got[t, s, step, :, :] = send[s, t, step, :, :]
-
-    @pl.when(step == planes - 1)
-    def _():
+        for k in range(len(offsets)):
+            copy(k).start()
+        got[t, s, :, :, :] = send[s, t, :, :, :]
         for a in range(times):
-            @pl.loop(0, planes)
-            def _(x):
-                for k in range(len(offsets)):
-                    if offsets[k][0] == a:
-                        arrival(x, k).wait_recv()
-                        copy(x, k).wait_send()
+            for k in range(len(offsets)):
+                if offsets[k][0] == a:
+                    arrival(k).wait_recv()
             from_t = lax.rem(t + times - a, times)
             rows = got[from_t].reshape(sources * planes * 8, LANES)
             finish_time(rows, line_ref, out_ref, from_t, own)
+        for k in range(len(offsets)):
+            copy(k).wait_send()
 
 
 def fast_device(prop_one, prop_two, times, sources):
@@ -442,8 +437,8 @@
             pltpu.VMEM((2, 16 * 2 * tiles, LANES), jnp.float32),
             pltpu.VMEM((sources, times, planes, 8, LANES), jnp.float32),
             pltpu.VMEM((times, sources, planes, 8, LANES), jnp.float32),
-            pltpu.SemaphoreType.DMA((planes, peers)),
-            pltpu.SemaphoreType.DMA((planes, peers)),
+            pltpu.SemaphoreType.DMA((peers,)),
+            pltpu.SemaphoreType.DMA((peers,)),
         ],
         compiler_params=pltpu.CompilerParams(
             collective_id=0, has_side_effects=True, dimension_semantics=("arbitrary",)

time: 27.9 us -> 28.1 us (level)
  no operation moved by 1% of the time
where the time goes in v2:
time: 28.1 us; the launch traced here: 27.9 us
  Pallas kernels  26 us (93%)
  local copies, waits for them, and re-layouts  1.89 us (7%)
    pallas_call x1, Pallas kernels, fast_device(): pl.pallas_call(functools.partial(fused_kernel, tables, tiles, planes, tim...  26 us
    unnamed x1, local copies, waits for them, and re-layouts  1.89 us

profile of v2, /device:TPU:0, one launch (start us, length us, event | category | flops | bytes accessed | tf_op | source)
XLA Modules:
  0.0 27.9 jit_solution(3436760599706790079)
XLA Ops:
  0.0 26.0 %shard_map.64 = f32[4,4,64,128]{3,2,1,0:T(8,128)} custom-call(bf16[12,12,64,128]{3,2,1,0:T(8,128)(2,1)} %bitcast.15, bf16[12,12,64,128]{3,2,1,0:T(8,128)(2,1)} %bitcast.16, f32[2,16,128]{2,1,0:T(8,128)} %constant.11.clone.phase_ref, f32[2,8,128]{2,1,0:T(8,128)} %constant.8.clone.twiddle_ref, bf16[2,256,256]{2,1,0:T(8,128)(2,1)} %constant.9.clone.plane_ref, ...), custom_call_target="tpu_custom_call" | custom-call | tf_op jit(solution)/shard_map/pallas_call | solution.py:428
  26.0 1.9 %copy.11 = f32[4,4,2,4096]{3,2,1,0:T(2,128)} copy(f32[4,4,2,4096]{3,2,1,0:T(2,128)} %bitcast.17) | data formatting | bytes 1048576
